TPU v7x, 32 devices: a whole 2x2x4 slice. The times are simulated.
32 devices in a mesh: gx: 4 (over x, core), gy: 4 (over z), gz: 2 (over y).
Axes of the slice: x: 2, y: 2, z: 4, core: 2. Of those that a mesh axis runs over, the one named last changes fastest.
Arguments:
- density: float32 [16, 128, 256], P('gx', 'gy', 'gz'), may hold values from 0.5 to 2
- velocity: float32 [3, 16, 128, 256], P(None, 'gx', 'gy', 'gz'), may hold values from -2.5 to 2.5
- pressure: float32 [16, 128, 256], P('gx', 'gy', 'gz'), may hold values from 0.5 to 2
Outputs:
- section_state: float32 [5, 16, 128, 256], P(None, 'gx', 'gy', 'gz')
All inputs are finite; a program needn't handle non-finite values.
Results may differ from a plain program's by a relative error of at most 0.0003.
Values sent between devices are 32-bit elements; how exact they have to be, the bound alone decides.
A program may use at most 64 MiB of HBM per device.

v0:
```python
import functools
import itertools
import math

import jax
import jax.numpy as jnp
from jax import lax
from jax.experimental import pallas as pl
from jax.experimental.pallas import tpu as pltpu
from jax.sharding import PartitionSpec as P

MESH = pl.DeviceIdType.MESH
AXES = ("gx", "gy", "gz")
gamma_gas = 1.4
weno_eps = 1e-06
cfl_number = 0.4
scale = 0.125
eps_outer = 0.75 * 16.0 * scale * scale * weno_eps
eps_inner = 0.75 * 4.0 * scale * scale * weno_eps
ROWS = 8
EARLY = 0


def rcp(x):
    guess = pl.reciprocal(x, approx=True)
    return guess * (2.0 - x * guess)


def cell_basis(rho, v, p):
    inv_root = lax.rsqrt(rho)
    c2 = gamma_gas * p * (inv_root * inv_root)
    m = [rho * u for u in v]
    energy = 2.5 * p + 0.5 * (m[0] * v[0] + m[1] * v[1] + m[2] * v[2])
    return rho, v, p, m, energy, rho * inv_root, c2, c2 * lax.rsqrt(c2)


def cell_arrays(basis, order):
    rho, v, p, m, energy, root, c2, sound = basis
    vn, va, vb = [v[k] for k in order]
    mn, ma, mb = [m[k] for k in order]
    return [
        rho, mn, ma, mb, energy,
        mn * vn + p, ma * vn, mb * vn, (energy + p) * vn,
        root, vn, va, vb, c2, jnp.abs(vn) + sound,
    ]


FIRST, SECOND, THIRD = (0, 1, 2), (1, 0, 2), (2, 0, 1)


def put_cells(ref, row, arrays):
    for k, array in enumerate(arrays):
        ref[k, pl.ds(row, array.shape[0]), :] = array


def weno(d1, d2, d3, d4, eps):
    h2 = (d2 + d2) - d1
    h3 = (d3 + d3) - d4
    e1, e2, e3 = d2 - d1, d3 - d2, d4 - d3
    s2, s3 = 0.75 * d2, 0.75 * d3
    a = (e1 * e1 + s2 * h2) + eps
    b = (e2 * e2 + s2 * d3) + eps
    c = (e3 * e3 + s3 * h3) + eps
    bc, ac, ab = b * c, a * c, a * b
    w0 = bc * bc
    w1 = 6.0 * (ac * ac)
    w2 = 1.5 * (ab * ab)
    den = w0 + w1 + (w2 + w2)
    return (w0 * (h2 - d3) + w2 * (h3 - d2)) * rcp(den)


def face_tile(cells, flux, base, stride, row):
    def load(k, j):
        return cells[k, pl.ds(base + j * stride, ROWS), :]

    sl, sr = load(9, 2), load(9, 3)
    inv = rcp(sl + sr)
    wl, wr = sl * inv, sr * inv
    vl = [load(10 + k, 2) for k in range(3)]
    dv = [load(10 + k, 3) - vl[k] for k in range(3)]
    un, ta, tb = [vl[k] + wr * dv[k] for k in range(3)]
    jump = dv[0] * dv[0] + dv[1] * dv[1] + dv[2] * dv[2]
    c2 = wl * load(13, 2) + wr * load(13, 3) + (0.2 * (wl * wr)) * jump
    ic = lax.rsqrt(c2)
    sound = c2 * ic
    b1 = 0.4 * (ic * ic)
    qh = 0.5 * (un * un + ta * ta + tb * tb)
    enth = 2.5 * c2 + qh
    alpha = load(14, 0)
    for j in range(1, 6):
        alpha = jnp.maximum(alpha, load(14, j))

    state = [[load(k, j) for j in range(6)] for k in range(5)]
    phys = [state[1]] + [[load(k, j) for j in range(6)] for k in range(5, 9)]
    du = [[s[j + 1] - s[j] for j in range(5)] for s in state]
    df = [du[1]] + [[s[j + 1] - s[j] for j in range(5)] for s in phys[1:]]
    au = [[alpha * d for d in s] for s in du]

    def project(r, mn, ma, mb, e):
        s = (un * r - mn) * ic
        z = b1 * (e - un * mn - ta * ma - tb * mb + qh * r)
        return z + s, r - z, ma - ta * r, mb - tb * r, z - s

    plus = [project(*[df[k][j] + au[k][j] for k in range(5)]) for j in range(4)]
    minus = [project(*[df[k][j] - au[k][j] for k in range(5)]) for j in range(1, 5)]
    hats = []
    for k in range(5):
        eps = eps_outer if k in (0, 4) else eps_inner
        up = weno(plus[0][k], plus[1][k], plus[2][k], plus[3][k], eps)
        down = weno(minus[3][k], minus[2][k], minus[1][k], minus[0][k], eps)
        hats.append(up - down)
    lin = []
    for k in range(5):
        centre = 6.0 * (phys[k][2] + phys[k][3]) + (df[k][1] - df[k][3])
        lin.append(centre + ((au[k][1] + au[k][3]) - (au[k][2] + au[k][2])))
    h1, h2, h3, h4, h5 = hats
    h2, h3, h4 = h2 + h2, h3 + h3, h4 + h4
    h15 = h1 + h5
    k5 = sound * (h5 - h1)
    s = h15 + h2
    result = [
        lin[0] + s,
        lin[1] + (un * s + k5),
        lin[2] + (ta * s + h3),
        lin[3] + (tb * s + h4),
        lin[4] + (enth * h15 + un * k5 + qh * h2 + ta * h3 + tb * h4),
    ]
    for k in range(5):
        flux[k, pl.ds(row, ROWS), :] = result[k]


def top_groups(counts):
    if math.prod(counts) <= 64:
        return (tuple(range(len(counts))),)
    return tuple((a,) for a in range(len(counts)))


def kernel(
    counts, early, den_in, vel_in, pre_in, out,
    den, vel, pre, cx, cy, cz, gx, gy, gz, acc, tz, hx, sy, hy, hz, top, got,
    in_sem, send_sem, recv_sem, top_send, top_recv,
):
    nx, ny, lanes = den.shape
    nrow = nx * ny
    nz = lanes
    tiles = ny // ROWS
    ypad = ny + 3 * ROWS
    yface = ny + ROWS

    me = [lax.axis_index(a) for a in AXES]
    barrier = pltpu.get_barrier_semaphore()
    groups = top_groups(counts)
    peers = []
    for stage, group in enumerate(groups):
        for shift in itertools.product(*(range(counts[a]) for a in group)):
            if any(shift):
                peer = {AXES[a]: lax.rem(me[a] + k, counts[a]) for a, k in zip(group, shift)}
                peers.append((stage, peer))
    for _, peer in peers:
        pl.semaphore_signal(barrier, inc=1, device_id=peer, device_id_type=MESH)

    pairs = ((den_in, den), (vel_in, vel), (pre_in, pre))
    loads = [pltpu.make_async_copy(a, b, in_sem.at[k]) for k, (a, b) in enumerate(pairs)]
    for copy in loads:
        copy.start()
    for copy in loads:
        copy.wait()

    def speeds(i, best):
        for t in range(tiles):
            r = t * ROWS
            inv_root = lax.rsqrt(den[i, pl.ds(r, ROWS), :])
            c2 = gamma_gas * pre[i, pl.ds(r, ROWS), :] * (inv_root * inv_root)
            v1, v2, v3 = [jnp.abs(vel[k, i, pl.ds(r, ROWS), :]) for k in range(3)]
            best = jnp.maximum(best, ((v1 + v2) + v3) + 3.0 * (c2 * lax.rsqrt(c2)))
        return best

    best = lax.fori_loop(0, nx, speeds, jnp.zeros((ROWS, lanes), jnp.float32))
    top[0] = jnp.max(best, axis=0, keepdims=True)

    def own_cells():
        @pl.loop(0, nx)
        def _(i):
            for t in range(tiles):
                r = t * ROWS
                rho = scale * den[i, pl.ds(r, ROWS), :]
                p = scale * pre[i, pl.ds(r, ROWS), :]
                basis = cell_basis(rho, [vel[k, i, pl.ds(r, ROWS), :] for k in range(3)], p)
                put_cells(cx, pl.multiple_of((3 + i) * ny + r, ROWS), cell_arrays(basis, FIRST))
                put_cells(cy, pl.multiple_of(i * ypad + ROWS + r, ROWS), cell_arrays(basis, SECOND))

    for side, start in ((0, ny - 3), (1, 0)):
        for i in range(nx):
            rows = [den[i, pl.ds(start, 3), :]]
            rows += [vel[k, i, pl.ds(start, 3), :] for k in range(3)]
            rows.append(pre[i, pl.ds(start, 3), :])
            for k in range(5):
                sy[side, pl.ds(3 * (k * nx + i), 3), :] = rows[k]

    tz[0] = den[...].reshape(nrow, nz).T
    for k in range(3):
        tz[1 + k] = vel[k].reshape(nrow, nz).T
    tz[4] = pre[...].reshape(nrow, nz).T

    def own_turned():
        @pl.loop(0, nz // ROWS, unroll=4)
        def _(t):
            r = pl.multiple_of(t * ROWS, ROWS)
            rho, v1, v2, v3, p = [tz[k, pl.ds(r, ROWS), :] for k in range(5)]
            basis = cell_basis(scale * rho, (v1, v2, v3), scale * p)
            put_cells(cz, r + ROWS, cell_arrays(basis, THIRD))

    def z_face(t):
        r = pl.multiple_of(t * ROWS, ROWS)
        face_tile(cz, gz, r + 5, 1, r)

    def y_face(i, t):
        face_tile(cy, gy, i * ypad + t * ROWS + 5, 1, pl.multiple_of(i * yface + t * ROWS, ROWS))

    if early >= 1:
        own_cells()
    if early >= 2:
        own_turned()

    pl.semaphore_wait(barrier, len(peers))

    def remote(src, dst, slot, peer):
        copy = pltpu.make_async_remote_copy(
            src_ref=src, dst_ref=dst, send_sem=send_sem.at[slot], recv_sem=recv_sem.at[slot],
            device_id=peer, device_id_type=MESH,
        )
        copy.start()
        return copy

    def send_top(axis):
        copies = []
        for slot, (other, peer) in enumerate(peers):
            if other == axis:
                copy = pltpu.make_async_remote_copy(
                    src_ref=top.at[axis], dst_ref=got.at[slot],
                    send_sem=top_send.at[slot], recv_sem=top_recv.at[slot],
                    device_id=peer, device_id_type=MESH,
                )
                copy.start()
                copies.append((slot, copy))
        return copies

    def take_top(axis, copies):
        best = top[axis]
        for slot, copy in copies:
            copy.wait()
            best = jnp.maximum(best, got[slot])
        top[axis + 1] = best

    def next_top(stage, copies):
        if stage >= len(groups) - 1:
            return copies
        take_top(stage, copies)
        return send_top(stage + 1)

    def near(axis, way):
        return {AXES[axis]: lax.rem(me[axis] + way + counts[axis], counts[axis])}

    pending = send_top(0)
    zc = [
        remote(tz.at[:, pl.ds(nz - ROWS, ROWS), :], hz.at[0], 0, near(2, 1)),
        remote(tz.at[:, pl.ds(0, ROWS), :], hz.at[1], 1, near(2, -1)),
    ]
    yc, xc = [], []
    for side, way in ((0, 1), (1, -1)):
        yc.append(remote(sy.at[side], hy.at[side], 2 + side, near(1, way)))
    for side, start, way in ((0, nx - 3, 1), (1, 0, -1)):
        peer = near(0, way)
        slot = 4 + 3 * side
        xc.append(remote(den.at[pl.ds(start, 3)], hx.at[side, 0], slot, peer))
        xc.append(remote(vel.at[:, pl.ds(start, 3)], hx.at[side, pl.ds(1, 3)], slot + 1, peer))
        xc.append(remote(pre.at[pl.ds(start, 3)], hx.at[side, 4], slot + 2, peer))

    if early < 1:
        own_cells()
    if early < 2:
        own_turned()
    pl.loop(1, nz // ROWS - 1)(z_face)
    pending = next_top(0, pending)

    @pl.loop(0, nx * (tiles - 2))
    def _(q):
        y_face(q // (tiles - 2), lax.rem(q, tiles - 2) + 1)

    pending = next_top(1, pending)

    for side, row in ((0, 0), (1, nz + ROWS)):
        zc[side].wait()
        rho, v1, v2, v3, p = [hz[side, k] for k in range(5)]
        put_cells(cz, row, cell_arrays(cell_basis(scale * rho, (v1, v2, v3), scale * p), THIRD))

    @pl.loop(0, 3)
    def _(t):
        z_face(jnp.where(t == 0, 0, nz // ROWS - 2 + t))

    for k, field in enumerate((0, 3, 1, 2, 4)):
        acc[field] = (gz[k, pl.ds(1, nz), :] - gz[k, pl.ds(0, nz), :]).T

    for copy in yc:
        copy.wait()
    for side in range(2):
        for i in range(nx):
            rho, v1, v2, v3, p = [hy[side, pl.ds(3 * (k * nx + i), 3), :] for k in range(5)]
            row = i * ypad + ROWS + (ny if side else -3)
            put_cells(cy, row, cell_arrays(cell_basis(scale * rho, (v1, v2, v3), scale * p), SECOND))

    @pl.loop(0, nx * 3)
    def _(q):
        t = lax.rem(q, 3)
        y_face(q // 3, jnp.where(t == 0, 0, tiles - 2 + t))

    pending = next_top(2, pending)

    for copy in xc:
        copy.wait()
    for side in range(2):
        @pl.loop(0, 3)
        def _(i):
            for t in range(tiles):
                r = t * ROWS
                rho, v1, v2, v3, p = [hx[side, k, i, pl.ds(r, ROWS), :] for k in range(5)]
                row = pl.multiple_of((side * (nx + 3) + i) * ny + r, ROWS)
                put_cells(cx, row, cell_arrays(cell_basis(scale * rho, (v1, v2, v3), scale * p), FIRST))

    @pl.loop(0, (nx + 1) * tiles)
    def _(q):
        r = pl.multiple_of(q * ROWS, ROWS)
        face_tile(cx, gx, r, ny, r)

    take_top(len(groups) - 1, pending)
    largest = jnp.max(top[len(groups)], axis=(0, 1), keepdims=True)
    factor = jnp.broadcast_to((cfl_number / (12.0 * scale)) / largest, (ROWS, lanes))

    @pl.loop(0, nx)
    def _(i):
        for t in range(tiles):
            r = t * ROWS
            row = pl.multiple_of(i * ny + r, ROWS)
            yrow = pl.multiple_of(i * yface + r, ROWS)
            for field, k in enumerate((0, 2, 1, 3, 4)):
                total = acc[field, pl.ds(row, ROWS), :]
                total = total + (gy[k, pl.ds(yrow + 1, ROWS), :] - gy[k, pl.ds(yrow, ROWS), :])
                total = total + (gx[field, pl.ds(row + ny, ROWS), :] - gx[field, pl.ds(row, ROWS), :])
                state = cx[field, pl.ds(pl.multiple_of(row + 3 * ny, ROWS), ROWS), :]
                out[field, i, pl.ds(r, ROWS), :] = (1.0 / scale) * state - factor * total


def local(counts, density, velocity, pressure):
    nx, ny, nz = density.shape
    nrow = nx * ny
    npeers = sum(math.prod(counts[a] for a in group) - 1 for group in top_groups(counts))
    f32 = jnp.float32
    vmem = pl.BlockSpec(memory_space=pltpu.VMEM)
    return pl.pallas_call(
        functools.partial(kernel, counts, EARLY),
        out_shape=pltpu.VMEM((5, nx, ny, nz), f32),
        in_specs=[pl.BlockSpec(memory_space=pl.ANY)] * 3,
        out_specs=vmem,
        scratch_shapes=[
            pltpu.VMEM((nx, ny, nz), f32),
            pltpu.VMEM((3, nx, ny, nz), f32),
            pltpu.VMEM((nx, ny, nz), f32),
            pltpu.VMEM((15, (nx + 6) * ny + ROWS, nz), f32),
            pltpu.VMEM((15, nx * (ny + 3 * ROWS) + ROWS, nz), f32),
            pltpu.VMEM((15, nz + 3 * ROWS, nrow), f32),
            pltpu.VMEM((5, (nx + 1) * ny, nz), f32),
            pltpu.VMEM((5, nx * (ny + ROWS), nz), f32),
            pltpu.VMEM((5, nz + ROWS, nrow), f32),
            pltpu.VMEM((5, nrow, nz), f32),
            pltpu.VMEM((5, nz, nrow), f32),
            pltpu.VMEM((2, 5, 3, ny, nz), f32),
            pltpu.VMEM((2, pl.cdiv(15 * nx, ROWS) * ROWS, nz), f32),
            pltpu.VMEM((2, pl.cdiv(15 * nx, ROWS) * ROWS, nz), f32),
            pltpu.VMEM((2, 5, ROWS, nrow), f32),
            pltpu.VMEM((4, 1, nz), f32),
            pltpu.VMEM((npeers, 1, nz), f32),
            pltpu.SemaphoreType.DMA((3,)),
            pltpu.SemaphoreType.DMA((10,)),
            pltpu.SemaphoreType.DMA((10,)),
            pltpu.SemaphoreType.DMA((npeers,)),
            pltpu.SemaphoreType.DMA((npeers,)),
        ],
        compiler_params=pltpu.CompilerParams(collective_id=0, has_side_effects=True),
    )(density, velocity, pressure)


def solution(mesh):
    counts = tuple(mesh.shape[a] for a in AXES)
    in_specs = (P("gx", "gy", "gz"), P(None, "gx", "gy", "gz"), P("gx", "gy", "gz"))
    out_specs = P(None, "gx", "gy", "gz")
    return jax.shard_map(
        functools.partial(local, counts), mesh=mesh, in_specs=in_specs, out_specs=out_specs, check_vma=False
    )
```

profile of v0, /device:TPU:1, one launch (start us, length us, event | category | flops | bytes accessed | tf_op | source)
XLA Modules:
  0.0 17.9 jit_solution(7635730363390120381)
XLA Ops:
  0.0 17.2 %shard_map.37 = f32[5,4,32,128]{3,2,1,0:T(8,128)S(1)} custom-call(f32[4,32,128]{2,1,0:T(8,128)} %den_in.1, f32[3,4,32,128]{3,2,1,0:T(8,128)} %vel_in.1, f32[4,32,128]{2,1,0:T(8,128)} %pre_in.1), custom_call_target="tpu_custom_call" | custom-call | tf_op jit(solution)/shard_map/pallas_call | solution.py:359
  17.2 0.7 %copy.5 = f32[5,4,32,128]{3,2,1,0:T(8,128)} copy(f32[5,4,32,128]{3,2,1,0:T(8,128)S(1)} %shard_map.37) | data formatting | bytes 655360
where the time goes:
time: 18.3 us; the launch traced here: 17.9 us
  Pallas kernels  17.2 us (94%)
  local copies, waits for them, and re-layouts  0.73 us (4%)
    pallas_call x1, Pallas kernels, local(): pl.pallas_call(functools.partial(kernel, counts, EARLY), out_shape=pltpu....  17.2 us
    unnamed x1, local copies, waits for them, and re-layouts  0.73 us

commit v1 on v0

v1 whole, which is shorter than its diff:
```python
import functools
import math

import jax
import jax.numpy as jnp
from jax import lax
from jax.experimental import pallas as pl
from jax.experimental.pallas import tpu as pltpu
from jax.sharding import PartitionSpec as P

MESH = pl.DeviceIdType.MESH
AXES = ("gx", "gy", "gz")
gamma_gas = 1.4
weno_eps = 1e-06
cfl_number = 0.4
scale = 0.125
eps_outer = 0.75 * 16.0 * scale * scale * weno_eps
eps_inner = 0.75 * 4.0 * scale * scale * weno_eps
ROWS = 8
AHEAD = 8


def rcp(x):
    guess = pl.reciprocal(x, approx=True)
    return guess * (2.0 - x * guess)


def cell_basis(rho, v, p):
    inv_root = lax.rsqrt(rho)
    c2 = gamma_gas * p * (inv_root * inv_root)
    m = [rho * u for u in v]
    energy = 2.5 * p + 0.5 * (m[0] * v[0] + m[1] * v[1] + m[2] * v[2])
    return rho, v, p, m, energy, rho * inv_root, c2, c2 * lax.rsqrt(c2)


def cell_arrays(basis, order):
    rho, v, p, m, energy, root, c2, sound = basis
    vn, va, vb = [v[k] for k in order]
    mn, ma, mb = [m[k] for k in order]
    return [
        rho, mn, ma, mb, energy,
        mn * vn + p, ma * vn, mb * vn, (energy + p) * vn,
        root, vn, va, vb, c2, jnp.abs(vn) + sound,
    ]


FIRST, SECOND, THIRD = (0, 1, 2), (1, 0, 2), (2, 0, 1)


def put_cells(ref, row, arrays):
    for k, array in enumerate(arrays):
        ref[k, pl.ds(row, array.shape[0]), :] = array


def weno(d1, d2, d3, d4, eps):
    h2 = (d2 + d2) - d1
    h3 = (d3 + d3) - d4
    e1, e2, e3 = d2 - d1, d3 - d2, d4 - d3
    s2, s3 = 0.75 * d2, 0.75 * d3
    a = (e1 * e1 + s2 * h2) + eps
    b = (e2 * e2 + s2 * d3) + eps
    c = (e3 * e3 + s3 * h3) + eps
    bc, ac, ab = b * c, a * c, a * b
    w0 = bc * bc
    w1 = 6.0 * (ac * ac)
    w2 = 1.5 * (ab * ab)
    den = w0 + w1 + (w2 + w2)
    return (w0 * (h2 - d3) + w2 * (h3 - d2)) * rcp(den)


def face_tile(cells, flux, base, stride, row, rows=ROWS, step=None):
    def load(k, j):
        return cells[k, pl.ds(base + j * stride, rows, step), :]

    sl, sr = load(9, 2), load(9, 3)
    inv = rcp(sl + sr)
    wl, wr = sl * inv, sr * inv
    vl = [load(10 + k, 2) for k in range(3)]
    dv = [load(10 + k, 3) - vl[k] for k in range(3)]
    un, ta, tb = [vl[k] + wr * dv[k] for k in range(3)]
    jump = dv[0] * dv[0] + dv[1] * dv[1] + dv[2] * dv[2]
    c2 = wl * load(13, 2) + wr * load(13, 3) + (0.2 * (wl * wr)) * jump
    ic = lax.rsqrt(c2)
    sound = c2 * ic
    b1 = 0.4 * (ic * ic)
    qh = 0.5 * (un * un + ta * ta + tb * tb)
    enth = 2.5 * c2 + qh
    alpha = load(14, 0)
    for j in range(1, 6):
        alpha = jnp.maximum(alpha, load(14, j))

    state = [[load(k, j) for j in range(6)] for k in range(5)]
    phys = [state[1]] + [[load(k, j) for j in range(6)] for k in range(5, 9)]
    du = [[s[j + 1] - s[j] for j in range(5)] for s in state]
    df = [du[1]] + [[s[j + 1] - s[j] for j in range(5)] for s in phys[1:]]
    au = [[alpha * d for d in s] for s in du]

    def project(r, mn, ma, mb, e):
        s = (un * r - mn) * ic
        z = b1 * (e - un * mn - ta * ma - tb * mb + qh * r)
        return z + s, r - z, ma - ta * r, mb - tb * r, z - s

    plus = [project(*[df[k][j] + au[k][j] for k in range(5)]) for j in range(4)]
    minus = [project(*[df[k][j] - au[k][j] for k in range(5)]) for j in range(1, 5)]
    hats = []
    for k in range(5):
        eps = eps_outer if k in (0, 4) else eps_inner
        up = weno(plus[0][k], plus[1][k], plus[2][k], plus[3][k], eps)
        down = weno(minus[3][k], minus[2][k], minus[1][k], minus[0][k], eps)
        hats.append(up - down)
    lin = []
    for k in range(5):
        centre = 6.0 * (phys[k][2] + phys[k][3]) + (df[k][1] - df[k][3])
        lin.append(centre + ((au[k][1] + au[k][3]) - (au[k][2] + au[k][2])))
    h1, h2, h3, h4, h5 = hats
    h2, h3, h4 = h2 + h2, h3 + h3, h4 + h4
    h15 = h1 + h5
    k5 = sound * (h5 - h1)
    s = h15 + h2
    result = [
        lin[0] + s,
        lin[1] + (un * s + k5),
        lin[2] + (ta * s + h3),
        lin[3] + (tb * s + h4),
        lin[4] + (enth * h15 + un * k5 + qh * h2 + ta * h3 + tb * h4),
    ]
    for k in range(5):
        flux[k, pl.ds(row, rows, step), :] = result[k]


def is_star(counts):
    return math.prod(counts) <= 64 and counts[0] >= 2 and counts[1] >= 3 and counts[2] >= 2


def kernel(
    counts, den_in, vel_in, pre_in, out,
    raw, cx, cy, cz, gx, gy, gz, acc, tz, hx, sy, hy, hz, top, got,
    in_sem, x_send, x_recv, y_send, y_recv, z_send, z_recv, top_send, top_recv, cast_send, cast_recv,
):
    nx, ny, lanes = raw.shape[1:]
    nrow = nx * ny
    nz = lanes
    tiles = ny // ROWS
    ypad = ny + 2 * ROWS
    devices = math.prod(counts)
    star = is_star(counts)

    pairs = ((den_in, raw.at[0]), (vel_in, raw.at[pl.ds(1, 3)]), (pre_in, raw.at[4]))
    loads = [pltpu.make_async_copy(a, b, in_sem.at[k]) for k, (a, b) in enumerate(pairs)]
    for copy in loads:
        copy.start()

    me = [lax.axis_index(a) for a in AXES]
    rank = (me[0] * counts[1] + me[1]) * counts[2] + me[2]
    roots = (0, counts[1] * counts[2])
    root = jnp.logical_and(me[0] <= 1, jnp.logical_and(me[1] == 0, me[2] == 0))
    odd = lax.rem(me[0], 2)
    last = me[1] == counts[1] - 1

    def device(d):
        return {
            "gx": lax.div(d, counts[1] * counts[2]),
            "gy": lax.rem(lax.div(d, counts[2]), counts[1]),
            "gz": lax.rem(d, counts[2]),
        }

    def near(axis, way):
        return {AXES[axis]: lax.rem(me[axis] + way + counts[axis], counts[axis])}

    barrier = pltpu.get_barrier_semaphore()

    def greet(peer):
        pl.semaphore_signal(barrier, inc=1, device_id=peer, device_id_type=MESH)

    if star:
        greeted = 2
        for axis in (0, 2):
            for way in sorted({1, counts[axis] - 1}):
                greet(near(axis, way))
                greeted += 1
        pl.when(me[1] > 0)(lambda: greet({"gy": me[1] - 1}))
        pl.when(me[1] < counts[1] - 1)(lambda: greet({"gy": me[1] + 1}))
        pl.when(me[1] == 0)(lambda: greet({"gy": counts[1] - 1}))
        greeted = greeted + jnp.where(me[1] == 0, 1, 2) - jnp.where(root, 1, 0)

        @pl.when(root)
        def _():
            @pl.loop(0, devices)
            def _(d):
                pl.when(d != rank)(lambda: greet(device(d)))
    else:
        peers = [(a, {AXES[a]: lax.rem(me[a] + k, counts[a])}) for a in range(3) for k in range(1, counts[a])]
        greeted = len(peers)
        for _, peer in peers:
            greet(peer)

    for copy in loads:
        copy.wait()

    def speeds(i, best):
        for t in range(tiles):
            r = t * ROWS
            inv_root = lax.rsqrt(raw[0, i, pl.ds(r, ROWS), :])
            c2 = gamma_gas * raw[4, i, pl.ds(r, ROWS), :] * (inv_root * inv_root)
            v1, v2, v3 = [jnp.abs(raw[1 + k, i, pl.ds(r, ROWS), :]) for k in range(3)]
            best = jnp.maximum(best, ((v1 + v2) + v3) + 3.0 * (c2 * lax.rsqrt(c2)))
        return best

    best = lax.fori_loop(0, nx, speeds, jnp.zeros((ROWS, lanes), jnp.float32))
    own = jnp.max(best, axis=0, keepdims=True)
    top[0] = own
    if star:
        got[rank] = own

    def own_cells():
        @pl.loop(0, nx)
        def _(i):
            for t in range(tiles):
                r = t * ROWS
                rho, v1, v2, v3, p = [raw[k, i, pl.ds(r, ROWS), :] for k in range(5)]
                basis = cell_basis(scale * rho, (v1, v2, v3), scale * p)
                put_cells(cx, pl.multiple_of((3 + i) * ny + r, ROWS), cell_arrays(basis, FIRST))
                put_cells(cy, pl.multiple_of(i * ypad + ROWS + r, ROWS), cell_arrays(basis, SECOND))

    def stage():
        for side, start in ((0, ny - 3), (1, 0)):
            for i in range(nx):
                for k in range(5):
                    sy[side, pl.ds(3 * (k * nx + i), 3), :] = raw[k, i, pl.ds(start, 3), :]
        for k in range(5):
            tz[k] = raw[k].reshape(nrow, nz).T

    def own_turned():
        @pl.loop(0, nz // ROWS, unroll=4)
        def _(t):
            r = pl.multiple_of(t * ROWS, ROWS)
            rho, v1, v2, v3, p = [tz[k, pl.ds(r, ROWS), :] for k in range(5)]
            basis = cell_basis(scale * rho, (v1, v2, v3), scale * p)
            put_cells(cz, r + ROWS, cell_arrays(basis, THIRD))

    def z_face(t):
        r = pl.multiple_of(t * ROWS, ROWS)
        face_tile(cz, gz, r + 5, 1, r)

    def y_face(i, t):
        face_tile(cy, gy, i * ypad + t * ROWS + 5, 1, pl.multiple_of(i * ypad + t * ROWS, ROWS))

    first = 1
    if star:
        ahead = min(AHEAD, nz // ROWS - 2)

        @pl.when(root)
        def _():
            stage()
            own_turned()
            pl.loop(1, 1 + ahead)(z_face)

        first = 1 + jnp.where(root, ahead, 0)

    pl.semaphore_wait(barrier, greeted)

    def remote(src, dst, send, recv, peer):
        return pltpu.make_async_remote_copy(
            src_ref=src, dst_ref=dst, send_sem=send, recv_sem=recv, device_id=peer, device_id_type=MESH
        )

    def to_root(k):
        return remote(top.at[0], got.at[rank], top_send.at[k], top_recv.at[rank], device(jnp.int32(roots[k])))

    def from_device(d):
        return remote(top.at[0], got.at[d], top_send.at[0], top_recv.at[d], device(d))

    def cast(d):
        return remote(top.at[1], top.at[2], cast_send.at[d], cast_recv.at[0], device(d))

    def exchange(axis):
        return [
            remote(top.at[axis], got.at[slot], top_send.at[slot], top_recv.at[slot], peer)
            for slot, (other, peer) in enumerate(peers) if other == axis
        ]

    def next_top(axis):
        best = top[axis]
        for copy in exchange(axis):
            copy.wait()
        for slot, (other, _) in enumerate(peers):
            if other == axis:
                best = jnp.maximum(best, got[slot])
        top[axis + 1] = best
        if axis < 2:
            for copy in exchange(axis + 1):
                copy.start()

    def x_copy(side, p):
        src = jnp.where(side == 0, nx - 1 - p, p)
        dst = jnp.where(side == 0, 2 - p, p)
        slot = 3 * side + p
        peer = near(0, jnp.where(side == 0, 1, -1))
        return remote(raw.at[:, src], hx.at[side, :, dst], x_send.at[slot], x_recv.at[slot], peer)

    def y_copy(side):
        return remote(sy.at[side], hy.at[side], y_send.at[side], y_recv.at[side], near(1, 1 - 2 * side))

    def z_copy(side):
        start = 0 if side else nz - ROWS
        src = tz.at[:, pl.ds(start, ROWS), :]
        return remote(src, hz.at[side], z_send.at[side], z_recv.at[side], near(2, 1 - 2 * side))

    if star:
        for k in range(2):
            pl.when(rank != roots[k])(lambda: to_root(k).start())
    else:
        for copy in exchange(0):
            copy.start()
    for p in range(3):
        x_copy(1 - odd, p).start()
    for p in range(3):
        x_copy(odd, p).start()
    if star:
        @pl.when(jnp.logical_not(root))
        def _():
            stage()
    else:
        stage()
    z_copy(0).start()
    z_copy(1).start()
    y_copy(0).start()
    if star:
        pl.when(me[1] > 0)(lambda: y_copy(1).start())
        pl.when(jnp.logical_not(root))(own_turned)
    else:
        y_copy(1).start()
        own_turned()
    own_cells()

    lax.fori_loop(first, nz // ROWS - 1, lambda t, c: (z_face(t), c)[1], 0)
    if not star:
        next_top(0)

    @pl.loop(0, nx * (tiles - 2))
    def _(q):
        y_face(q // (tiles - 2), lax.rem(q, tiles - 2) + 1)

    if not star:
        next_top(1)

    def x_plane(side, p):
        x_copy(side, p).wait_recv()
        j = jnp.where(side == 0, 2 - p, p)
        base = jnp.where(side == 0, 2 - p, nx + 3 + p) * ny
        for t in range(tiles):
            r = t * ROWS
            rho, v1, v2, v3, pr = [hx[side, k, j, pl.ds(r, ROWS), :] for k in range(5)]
            basis = cell_basis(scale * rho, (v1, v2, v3), scale * pr)
            put_cells(cx, pl.multiple_of(base + r, ROWS), cell_arrays(basis, FIRST))

    def x_faces(start, number):
        @pl.loop(0, number * tiles)
        def _(q):
            r = pl.multiple_of(start * ny + q * ROWS, ROWS)
            face_tile(cx, gx, r, ny, r)

    pl.loop(0, 3)(lambda p: x_plane(1 - odd, p))
    x_faces(jnp.where(odd == 1, 0, 3), nx - 2)

    for side, row in ((0, 0), (1, nz + ROWS)):
        z_copy(side).wait_recv()
        rho, v1, v2, v3, p = [hz[side, k] for k in range(5)]
        put_cells(cz, row, cell_arrays(cell_basis(scale * rho, (v1, v2, v3), scale * p), THIRD))

    @pl.loop(0, 3)
    def _(t):
        z_face(jnp.where(t == 0, 0, nz // ROWS - 2 + t))

    for k, field in enumerate((0, 3, 1, 2, 4)):
        acc[field] = (gz[k, pl.ds(1, nz), :] - gz[k, pl.ds(0, nz), :]).T

    def y_side(side):
        y_copy(side).wait_recv()
        if side == 0 and star:
            pl.when(me[1] == 0)(lambda: y_copy(1).start())
        for i in range(nx):
            rho, v1, v2, v3, p = [hy[side, pl.ds(3 * (k * nx + i), 3), :] for k in range(5)]
            row = i * ypad + ROWS + (ny if side else -3)
            put_cells(cy, row, cell_arrays(cell_basis(scale * rho, (v1, v2, v3), scale * p), SECOND))

        @pl.loop(0, nx)
        def _(i):
            y_face(i, (tiles - 1) * side)

    def x_next(p):
        x_plane(odd, p)
        x_faces(jnp.where(odd == 1, nx - 2 + p, 2 - p), 1)

    pl.when(last)(lambda: y_side(0))
    pl.when(jnp.logical_not(last))(lambda: y_side(1))
    pl.loop(0, 2)(x_next)
    pl.when(last)(lambda: y_side(1))
    pl.when(jnp.logical_not(last))(lambda: y_side(0))
    face_tile(cy, gy, ny + 5, 1, ny, nx, ypad)

    @pl.loop(0, nx)
    def _(i):
        for t in range(tiles):
            r = t * ROWS
            row = pl.multiple_of(i * ny + r, ROWS)
            yrow = pl.multiple_of(i * ypad + r, ROWS)
            for field, k in enumerate((0, 2, 1, 3, 4)):
                turn = gy[k, pl.ds(yrow + 1, ROWS), :] - gy[k, pl.ds(yrow, ROWS), :]
                acc[field, pl.ds(row, ROWS), :] = acc[field, pl.ds(row, ROWS), :] + turn

    def gather(k):
        @pl.when(rank == roots[k])
        def _():
            @pl.loop(0, devices)
            def _(d):
                pl.when(d != rank)(lambda: from_device(d).wait_recv())

            best = jnp.max(got[...], axis=0)
            top[1] = best
            top[2] = best
            if k == 1:
                @pl.loop(1, devices)
                def _(d):
                    pl.when(d != rank)(lambda: cast(d).start())

    if star:
        gather(1)
    else:
        next_top(2)
    x_next(2)
    if star:
        gather(0)

    @pl.loop(0, nx)
    def _(i):
        for t in range(tiles):
            row = pl.multiple_of(i * ny + t * ROWS, ROWS)
            for field in range(5):
                turn = gx[field, pl.ds(row + ny, ROWS), :] - gx[field, pl.ds(row, ROWS), :]
                acc[field, pl.ds(row, ROWS), :] = acc[field, pl.ds(row, ROWS), :] + turn

    if star:
        pl.when(jnp.logical_not(root))(lambda: cast(rank).wait_recv())
    largest = jnp.max(top[2 if star else 3], axis=(0, 1), keepdims=True)
    factor = jnp.broadcast_to((cfl_number / (12.0 * scale)) / largest, (ROWS, lanes))

    @pl.loop(0, nx)
    def _(i):
        for t in range(tiles):
            r = t * ROWS
            row = pl.multiple_of(i * ny + r, ROWS)
            for field in range(5):
                state = cx[field, pl.ds(pl.multiple_of(row + 3 * ny, ROWS), ROWS), :]
                out[field, i, pl.ds(r, ROWS), :] = (1.0 / scale) * state - factor * acc[field, pl.ds(row, ROWS), :]

    if star:
        for k in range(2):
            pl.when(rank != roots[k])(lambda: to_root(k).wait_send())

        @pl.when(rank == roots[1])
        def _():
            @pl.loop(1, devices)
            def _(d):
                pl.when(d != rank)(lambda: cast(d).wait_send())
    for side in range(2):
        for p in range(3):
            x_copy(side, p).wait_send()
        y_copy(side).wait_send()
        z_copy(side).wait_send()


def local(counts, density, velocity, pressure):
    nx, ny, nz = density.shape
    nrow = nx * ny
    slots = math.prod(counts) if is_star(counts) else sum(counts) - 3
    casts = slots if is_star(counts) else 1
    f32 = jnp.float32
    vmem = pl.BlockSpec(memory_space=pltpu.VMEM)
    edge = pl.cdiv(15 * nx, ROWS) * ROWS
    return pl.pallas_call(
        functools.partial(kernel, counts),
        out_shape=pltpu.VMEM((5, nx, ny, nz), f32),
        in_specs=[pl.BlockSpec(memory_space=pl.ANY)] * 3,
        out_specs=vmem,
        scratch_shapes=[
            pltpu.VMEM((5, nx, ny, nz), f32),
            pltpu.VMEM((15, (nx + 6) * ny + ROWS, nz), f32),
            pltpu.VMEM((15, nx * (ny + 2 * ROWS) + ROWS, nz), f32),
            pltpu.VMEM((15, nz + 3 * ROWS, nrow), f32),
            pltpu.VMEM((5, (nx + 1) * ny, nz), f32),
            pltpu.VMEM((5, nx * (ny + 2 * ROWS), nz), f32),
            pltpu.VMEM((5, nz + ROWS, nrow), f32),
            pltpu.VMEM((5, nrow, nz), f32),
            pltpu.VMEM((5, nz, nrow), f32),
            pltpu.VMEM((2, 5, 3, ny, nz), f32),
            pltpu.VMEM((2, edge, nz), f32),
            pltpu.VMEM((2, edge, nz), f32),
            pltpu.VMEM((2, 5, ROWS, nrow), f32),
            pltpu.VMEM((4, 1, nz), f32),
            pltpu.VMEM((slots, 1, nz), f32),
            pltpu.SemaphoreType.DMA((3,)),
            pltpu.SemaphoreType.DMA((6,)),
            pltpu.SemaphoreType.DMA((6,)),
            pltpu.SemaphoreType.DMA((2,)),
            pltpu.SemaphoreType.DMA((2,)),
            pltpu.SemaphoreType.DMA((2,)),
            pltpu.SemaphoreType.DMA((2,)),
            pltpu.SemaphoreType.DMA((slots,)),
            pltpu.SemaphoreType.DMA((slots,)),
            pltpu.SemaphoreType.DMA((casts,)),
            pltpu.SemaphoreType.DMA((1,)),
        ],
        compiler_params=pltpu.CompilerParams(collective_id=0, has_side_effects=True),
    )(density, velocity, pressure)


def solution(mesh):
    counts = tuple(mesh.shape[a] for a in AXES)
    in_specs = (P("gx", "gy", "gz"), P(None, "gx", "gy", "gz"), P("gx", "gy", "gz"))
    out_specs = P(None, "gx", "gy", "gz")
    return jax.shard_map(
        functools.partial(local, counts), mesh=mesh, in_specs=in_specs, out_specs=out_specs, check_vma=False
    )
```

time: 18.3 us -> 14.2 us (0.78); the launches traced: 17.9 us -> 14.1 us
  Pallas kernels: 17.2 us -> 13.3 us
    pallas_call x1, Pallas kernels: 17.2 us -> 13.3 us  [local(): pl.pallas_call(functools.partial(kernel, counts), out_shape=pltpu.VMEM((5...]
where the time goes in v1:
time: 14.2 us; the launch traced here: 14.1 us
  Pallas kernels  13.3 us (94%)
  local copies, waits for them, and re-layouts  0.73 us (5%)
    pallas_call x1, Pallas kernels, local(): pl.pallas_call(functools.partial(kernel, counts), out_shape=pltpu.VMEM((5...  13.3 us
    unnamed x1, local copies, waits for them, and re-layouts  0.73 us

profile of v1, /device:TPU:1, one launch (start us, length us, event | category | flops | bytes accessed | tf_op | source)
XLA Modules:
  0.0 14.1 jit_solution(3737105265005508931)
XLA Ops:
  0.0 13.3 %shard_map.37 = f32[5,4,32,128]{3,2,1,0:T(8,128)S(1)} custom-call(f32[4,32,128]{2,1,0:T(8,128)} %den_in.1, f32[3,4,32,128]{3,2,1,0:T(8,128)} %vel_in.1, f32[4,32,128]{2,1,0:T(8,128)} %pre_in.1), custom_call_target="tpu_custom_call" | custom-call | tf_op jit(solution)/shard_map/pallas_call | solution.py:481
  13.3 0.7 %copy.5 = f32[5,4,32,128]{3,2,1,0:T(8,128)} copy(f32[5,4,32,128]{3,2,1,0:T(8,128)S(1)} %shard_map.37) | data formatting | bytes 655360

commit v2 on v1

--- a/solution.py
+++ b/solution.py
@@ -21,8 +21,7 @@
 
 
 def rcp(x):
-    guess = pl.reciprocal(x, approx=True)
-    return guess * (2.0 - x * guess)
+    return pl.reciprocal(x)
 
 
 def cell_basis(rho, v, p):
@@ -53,19 +52,18 @@
 
 
 def weno(d1, d2, d3, d4, eps):
-    h2 = (d2 + d2) - d1
-    h3 = (d3 + d3) - d4
     e1, e2, e3 = d2 - d1, d3 - d2, d4 - d3
     s2, s3 = 0.75 * d2, 0.75 * d3
-    a = (e1 * e1 + s2 * h2) + eps
-    b = (e2 * e2 + s2 * d3) + eps
-    c = (e3 * e3 + s3 * h3) + eps
+    q2, q3 = s2 * d2 + eps, s3 * d3 + eps
+    a = e1 * (e1 + s2) + q2
+    b = e2 * (e2 + s2) + q2
+    c = e3 * (e3 - s3) + q3
     bc, ac, ab = b * c, a * c, a * b
     w0 = bc * bc
     w1 = 6.0 * (ac * ac)
     w2 = 1.5 * (ab * ab)
     den = w0 + w1 + (w2 + w2)
-    return (w0 * (h2 - d3) + w2 * (h3 - d2)) * rcp(den)
+    return (w0 * (e1 - e2) + w2 * (e2 - e3)) * rcp(den)
 
 
 def face_tile(cells, flux, base, stride, row, rows=ROWS, step=None):
@@ -129,13 +127,13 @@
 
 
 def is_star(counts):
-    return math.prod(counts) <= 64 and counts[0] >= 2 and counts[1] >= 3 and counts[2] >= 2
+    return math.prod(counts) <= 64 and counts[0] >= 4 and counts[1] >= 3 and counts[2] == 2
 
 
 def kernel(
     counts, den_in, vel_in, pre_in, out,
     raw, cx, cy, cz, gx, gy, gz, acc, tz, hx, sy, hy, hz, top, got,
-    in_sem, x_send, x_recv, y_send, y_recv, z_send, z_recv, top_send, top_recv, cast_send, cast_recv,
+    in_sem, x_send, x_recv, y_send, y_recv, z_send, z_recv, top_send, top_recv, cast_send, cast_recv, permit,
 ):
     nx, ny, lanes = raw.shape[1:]
     nrow = nx * ny
@@ -146,9 +144,8 @@
     star = is_star(counts)
 
     pairs = ((den_in, raw.at[0]), (vel_in, raw.at[pl.ds(1, 3)]), (pre_in, raw.at[4]))
-    loads = [pltpu.make_async_copy(a, b, in_sem.at[k]) for k, (a, b) in enumerate(pairs)]
-    for copy in loads:
-        copy.start()
+    for a, b in pairs:
+        pltpu.make_async_copy(a, b, in_sem).start()
 
     me = [lax.axis_index(a) for a in AXES]
     rank = (me[0] * counts[1] + me[1]) * counts[2] + me[2]
@@ -172,30 +169,29 @@
     def greet(peer):
         pl.semaphore_signal(barrier, inc=1, device_id=peer, device_id_type=MESH)
 
-    if star:
-        greeted = 2
-        for axis in (0, 2):
-            for way in sorted({1, counts[axis] - 1}):
-                greet(near(axis, way))
-                greeted += 1
-        pl.when(me[1] > 0)(lambda: greet({"gy": me[1] - 1}))
-        pl.when(me[1] < counts[1] - 1)(lambda: greet({"gy": me[1] + 1}))
-        pl.when(me[1] == 0)(lambda: greet({"gy": counts[1] - 1}))
-        greeted = greeted + jnp.where(me[1] == 0, 1, 2) - jnp.where(root, 1, 0)
+    ends = me[1] == 0, last
+    lower = me[2] == 0
+    if star:
+        greet(near(0, 1))
+        greet(near(0, -1))
+        pl.when(jnp.logical_not(last))(lambda: greet(near(1, 1)))
+        pl.when(ends[0])(lambda: greet(near(1, -1)))
+        pl.when(lower)(lambda: greet(near(2, 1)))
 
         @pl.when(root)
         def _():
             @pl.loop(0, devices)
             def _(d):
                 pl.when(d != rank)(lambda: greet(device(d)))
+
+        greeted = 4 + jnp.where(ends[0], 0, 1) + jnp.where(last, 1, 0) + jnp.where(lower, 0, 1) - jnp.where(root, 1, 0)
     else:
         peers = [(a, {AXES[a]: lax.rem(me[a] + k, counts[a])}) for a in range(3) for k in range(1, counts[a])]
         greeted = len(peers)
         for _, peer in peers:
             greet(peer)
 
-    for copy in loads:
-        copy.wait()
+    pltpu.make_async_copy(raw, raw, in_sem).wait()
 
     def speeds(i, best):
         for t in range(tiles):
@@ -245,17 +241,27 @@
     def y_face(i, t):
         face_tile(cy, gy, i * ypad + t * ROWS + 5, 1, pl.multiple_of(i * ypad + t * ROWS, ROWS))
 
-    first = 1
-    if star:
-        ahead = min(AHEAD, nz // ROWS - 2)
+    def pairs_of(body, start, number):
+        @pl.loop(0, number // 2)
+        def _(q):
+            body(start + 2 * q)
+            body(start + 2 * q + 1)
+
+        if number % 2:
+            body(start + number - 1)
+
+    inside = nz // ROWS - 2
+    first = 0
+    if star:
+        ahead = min(AHEAD, inside) // 2
 
         @pl.when(root)
         def _():
             stage()
             own_turned()
-            pl.loop(1, 1 + ahead)(z_face)
-
-        first = 1 + jnp.where(root, ahead, 0)
+            pairs_of(z_face, 1, 2 * ahead)
+
+        first = jnp.where(root, ahead, 0)
 
     pl.semaphore_wait(barrier, greeted)
 
@@ -265,13 +271,14 @@
         )
 
     def to_root(k):
-        return remote(top.at[0], got.at[rank], top_send.at[k], top_recv.at[rank], device(jnp.int32(roots[k])))
-
-    def from_device(d):
-        return remote(top.at[0], got.at[d], top_send.at[0], top_recv.at[d], device(d))
+        return remote(top.at[0], got.at[rank], top_send, top_recv, device(jnp.int32(roots[k])))
 
     def cast(d):
-        return remote(top.at[1], top.at[2], cast_send.at[d], cast_recv.at[0], device(d))
+        return remote(top.at[1], top.at[2], cast_send, cast_recv, device(jnp.int32(d)))
+
+    def slots(number, send, recv):
+        part = got.at[pl.ds(0, number)]
+        return remote(part, part, send, recv, near(0, 1))
 
     def exchange(axis):
         return [
@@ -291,20 +298,26 @@
             for copy in exchange(axis + 1):
                 copy.start()
 
-    def x_copy(side, p):
+    def x_far(side, p):
         src = jnp.where(side == 0, nx - 1 - p, p)
         dst = jnp.where(side == 0, 2 - p, p)
-        slot = 3 * side + p
         peer = near(0, jnp.where(side == 0, 1, -1))
-        return remote(raw.at[:, src], hx.at[side, :, dst], x_send.at[slot], x_recv.at[slot], peer)
+        return remote(raw.at[:, src], hx.at[side, :, dst], x_send, x_recv.at[p], peer)
+
+    def x_near(side):
+        src = raw.at[:, pl.ds(jnp.where(side == 0, nx - 3, 0), 3)]
+        return remote(src, hx.at[side], x_send, x_recv.at[3], near(0, jnp.where(side == 0, 1, -1)))
 
     def y_copy(side):
-        return remote(sy.at[side], hy.at[side], y_send.at[side], y_recv.at[side], near(1, 1 - 2 * side))
-
-    def z_copy(side):
-        start = 0 if side else nz - ROWS
-        src = tz.at[:, pl.ds(start, ROWS), :]
-        return remote(src, hz.at[side], z_send.at[side], z_recv.at[side], near(2, 1 - 2 * side))
+        return remote(sy.at[side], hy.at[side], y_send, y_recv.at[side], near(1, 1 - 2 * side))
+
+    def z_copies():
+        for side, start in ((0, nz - ROWS), (1, 0)):
+            src = tz.at[:, pl.ds(start, ROWS), :]
+            remote(src, hz.at[side], z_send, z_recv, near(2, 1 - 2 * side)).start()
+
+    def allow(which, peer):
+        pl.semaphore_signal(permit.at[which], inc=1, device_id=peer, device_id_type=MESH)
 
     if star:
         for k in range(2):
@@ -313,39 +326,51 @@
         for copy in exchange(0):
             copy.start()
     for p in range(3):
-        x_copy(1 - odd, p).start()
-    for p in range(3):
-        x_copy(odd, p).start()
-    if star:
+        x_far(1 - odd, p).start()
+    x_near(odd).start()
+    if star:
+        pl.when(jnp.logical_not(ends[0]))(lambda: allow(0, near(1, -1)))
+        pl.when(jnp.logical_not(lower))(lambda: allow(0, near(2, -1)))
+        pl.when(last)(lambda: allow(1, near(1, 1)))
+
         @pl.when(jnp.logical_not(root))
         def _():
             stage()
+
+        pl.when(last)(lambda: y_copy(0).start())
+        pl.when(jnp.logical_not(ends[0]))(lambda: y_copy(1).start())
+        pl.when(jnp.logical_not(lower))(z_copies)
+        pl.when(jnp.logical_not(root))(own_turned)
     else:
         stage()
-    z_copy(0).start()
-    z_copy(1).start()
-    y_copy(0).start()
-    if star:
-        pl.when(me[1] > 0)(lambda: y_copy(1).start())
-        pl.when(jnp.logical_not(root))(own_turned)
-    else:
+        z_copies()
+        y_copy(0).start()
         y_copy(1).start()
         own_turned()
     own_cells()
 
-    lax.fori_loop(first, nz // ROWS - 1, lambda t, c: (z_face(t), c)[1], 0)
+    def z_pair(q, carry):
+        z_face(1 + 2 * q)
+        z_face(2 + 2 * q)
+        return carry
+
+    lax.fori_loop(first, inside // 2, z_pair, 0)
+    if inside % 2:
+        z_face(inside)
+    if star:
+        needed = jnp.where(last, 0, 1) + jnp.where(lower, 1, 0)
+        pl.when(needed > 0)(lambda: pl.semaphore_wait(permit.at[0], needed))
+        pl.when(lower)(z_copies)
+        pl.when(jnp.logical_not(last))(lambda: y_copy(0).start())
     if not star:
         next_top(0)
 
-    @pl.loop(0, nx * (tiles - 2))
-    def _(q):
-        y_face(q // (tiles - 2), lax.rem(q, tiles - 2) + 1)
+    pairs_of(lambda q: y_face(q // (tiles - 2), lax.rem(q, tiles - 2) + 1), 0, nx * (tiles - 2))
 
     if not star:
         next_top(1)
 
     def x_plane(side, p):
-        x_copy(side, p).wait_recv()
         j = jnp.where(side == 0, 2 - p, p)
         base = jnp.where(side == 0, 2 - p, nx + 3 + p) * ny
         for t in range(tiles):
@@ -355,16 +380,24 @@
             put_cells(cx, pl.multiple_of(base + r, ROWS), cell_arrays(basis, FIRST))
 
     def x_faces(start, number):
-        @pl.loop(0, number * tiles)
-        def _(q):
+        def x_face(q):
             r = pl.multiple_of(start * ny + q * ROWS, ROWS)
             face_tile(cx, gx, r, ny, r)
 
+        pairs_of(x_face, 0, number * tiles)
+
+    x_near(1 - odd).wait_recv()
     pl.loop(0, 3)(lambda p: x_plane(1 - odd, p))
     x_faces(jnp.where(odd == 1, 0, 3), nx - 2)
 
+    if star:
+        @pl.when(ends[0])
+        def _():
+            pl.semaphore_wait(permit.at[1], 1)
+            y_copy(1).start()
+
+    remote(hz, hz, z_send, z_recv, near(2, 1)).wait_recv()
     for side, row in ((0, 0), (1, nz + ROWS)):
-        z_copy(side).wait_recv()
         rho, v1, v2, v3, p = [hz[side, k] for k in range(5)]
         put_cells(cz, row, cell_arrays(cell_basis(scale * rho, (v1, v2, v3), scale * p), THIRD))
 
@@ -377,18 +410,15 @@
 
     def y_side(side):
         y_copy(side).wait_recv()
-        if side == 0 and star:
-            pl.when(me[1] == 0)(lambda: y_copy(1).start())
         for i in range(nx):
             rho, v1, v2, v3, p = [hy[side, pl.ds(3 * (k * nx + i), 3), :] for k in range(5)]
             row = i * ypad + ROWS + (ny if side else -3)
             put_cells(cy, row, cell_arrays(cell_basis(scale * rho, (v1, v2, v3), scale * p), SECOND))
 
-        @pl.loop(0, nx)
-        def _(i):
-            y_face(i, (tiles - 1) * side)
+        pairs_of(lambda i: y_face(i, (tiles - 1) * side), 0, nx)
 
     def x_next(p):
+        x_far(odd, p).wait_recv()
         x_plane(odd, p)
         x_faces(jnp.where(odd == 1, nx - 2 + p, 2 - p), 1)
 
@@ -412,17 +442,14 @@
     def gather(k):
         @pl.when(rank == roots[k])
         def _():
-            @pl.loop(0, devices)
-            def _(d):
-                pl.when(d != rank)(lambda: from_device(d).wait_recv())
-
+            slots(devices - 1, top_send, top_recv).wait_recv()
             best = jnp.max(got[...], axis=0)
             top[1] = best
             top[2] = best
             if k == 1:
-                @pl.loop(1, devices)
-                def _(d):
-                    pl.when(d != rank)(lambda: cast(d).start())
+                for d in reversed(range(devices)):
+                    if d not in roots:
+                        cast(d).start()
 
     if star:
         gather(1)
@@ -441,7 +468,7 @@
                 acc[field, pl.ds(row, ROWS), :] = acc[field, pl.ds(row, ROWS), :] + turn
 
     if star:
-        pl.when(jnp.logical_not(root))(lambda: cast(rank).wait_recv())
+        pl.when(jnp.logical_not(root))(lambda: cast(0).wait_recv())
     largest = jnp.max(top[2 if star else 3], axis=(0, 1), keepdims=True)
     factor = jnp.broadcast_to((cfl_number / (12.0 * scale)) / largest, (ROWS, lanes))
 
@@ -455,26 +482,19 @@
                 out[field, i, pl.ds(r, ROWS), :] = (1.0 / scale) * state - factor * acc[field, pl.ds(row, ROWS), :]
 
     if star:
-        for k in range(2):
-            pl.when(rank != roots[k])(lambda: to_root(k).wait_send())
-
-        @pl.when(rank == roots[1])
-        def _():
-            @pl.loop(1, devices)
-            def _(d):
-                pl.when(d != rank)(lambda: cast(d).wait_send())
-    for side in range(2):
-        for p in range(3):
-            x_copy(side, p).wait_send()
-        y_copy(side).wait_send()
-        z_copy(side).wait_send()
+        pl.when(root)(lambda: slots(1, top_send, top_recv).wait_send())
+        pl.when(jnp.logical_not(root))(lambda: slots(2, top_send, top_recv).wait_send())
+        pl.when(rank == roots[1])(lambda: slots(devices - 2, cast_send, cast_recv).wait_send())
+    remote(hx, hx, x_send, x_recv.at[0], near(0, 1)).wait_send()
+    remote(sy, sy, y_send, y_recv.at[0], near(1, 1)).wait_send()
+    remote(hz, hz, z_send, z_recv, near(2, 1)).wait_send()
 
 
 def local(counts, density, velocity, pressure):
     nx, ny, nz = density.shape
     nrow = nx * ny
     slots = math.prod(counts) if is_star(counts) else sum(counts) - 3
-    casts = slots if is_star(counts) else 1
+    hands = [pltpu.SemaphoreType.DMA if is_star(counts) else pltpu.SemaphoreType.DMA((slots,))] * 2
     f32 = jnp.float32
     vmem = pl.BlockSpec(memory_space=pltpu.VMEM)
     edge = pl.cdiv(15 * nx, ROWS) * ROWS
@@ -499,17 +519,17 @@
             pltpu.VMEM((2, 5, ROWS, nrow), f32),
             pltpu.VMEM((4, 1, nz), f32),
             pltpu.VMEM((slots, 1, nz), f32),
-            pltpu.SemaphoreType.DMA((3,)),
-            pltpu.SemaphoreType.DMA((6,)),
-            pltpu.SemaphoreType.DMA((6,)),
+            pltpu.SemaphoreType.DMA,
+            pltpu.SemaphoreType.DMA,
+            pltpu.SemaphoreType.DMA((4,)),
+            pltpu.SemaphoreType.DMA,
             pltpu.SemaphoreType.DMA((2,)),
-            pltpu.SemaphoreType.DMA((2,)),
-            pltpu.SemaphoreType.DMA((2,)),
-            pltpu.SemaphoreType.DMA((2,)),
-            pltpu.SemaphoreType.DMA((slots,)),
-            pltpu.SemaphoreType.DMA((slots,)),
-            pltpu.SemaphoreType.DMA((casts,)),
-            pltpu.SemaphoreType.DMA((1,)),
+            pltpu.SemaphoreType.DMA,
+            pltpu.SemaphoreType.DMA,
+            *hands,
+            pltpu.SemaphoreType.DMA,
+            pltpu.SemaphoreType.DMA,
+            pltpu.SemaphoreType.REGULAR((2,)),
         ],
         compiler_params=pltpu.CompilerParams(collective_id=0, has_side_effects=True),
     )(density, velocity, pressure)

time: 14.2 us -> 11.8 us (0.83)
  Pallas kernels: 13.3 us -> 11 us
    pallas_call x1, Pallas kernels: 13.3 us -> 11 us  [local(): pl.pallas_call(functools.partial(kernel, counts), out_shape=pltpu.VMEM((5...]
where the time goes in v2:
time: 11.8 us; the launch traced here: 11.7 us
  Pallas kernels  11 us (93%)
  local copies, waits for them, and re-layouts  0.73 us (6%)
    pallas_call x1, Pallas kernels, local(): pl.pallas_call(functools.partial(kernel, counts), out_shape=pltpu.VMEM((5...  11 us
    unnamed x1, local copies, waits for them, and re-layouts  0.73 us

profile of v2, /device:TPU:1, one launch (start us, length us, event | category | flops | bytes accessed | tf_op | source)
XLA Modules:
  0.0 11.7 jit_solution(3471570948336456918)
XLA Ops:
  0.0 11.0 %shard_map.37 = f32[5,4,32,128]{3,2,1,0:T(8,128)S(1)} custom-call(f32[4,32,128]{2,1,0:T(8,128)} %den_in.1, f32[3,4,32,128]{3,2,1,0:T(8,128)} %vel_in.1, f32[4,32,128]{2,1,0:T(8,128)} %pre_in.1), custom_call_target="tpu_custom_call" | custom-call | tf_op jit(solution)/shard_map/pallas_call | solution.py:501
  11.0 0.7 %copy.5 = f32[5,4,32,128]{3,2,1,0:T(8,128)} copy(f32[5,4,32,128]{3,2,1,0:T(8,128)S(1)} %shard_map.37) | data formatting | bytes 655360

commit v3 on v2

--- a/solution.py
+++ b/solution.py
@@ -132,7 +132,7 @@
 
 def kernel(
     counts, den_in, vel_in, pre_in, out,
-    raw, cx, cy, cz, gx, gy, gz, acc, tz, hx, sy, hy, hz, top, got,
+    raw, cx, cy, cz, gx, gy, gz, acc, tz, hx, sy, hy, sz, hz, top, got,
     in_sem, x_send, x_recv, y_send, y_recv, z_send, z_recv, top_send, top_recv, cast_send, cast_recv, permit,
 ):
     nx, ny, lanes = raw.shape[1:]
@@ -140,6 +140,7 @@
     nz = lanes
     tiles = ny // ROWS
     ypad = ny + 2 * ROWS
+    half = ny // 2
     devices = math.prod(counts)
     star = is_star(counts)
 
@@ -225,6 +226,9 @@
                     sy[side, pl.ds(3 * (k * nx + i), 3), :] = raw[k, i, pl.ds(start, 3), :]
         for k in range(5):
             tz[k] = raw[k].reshape(nrow, nz).T
+        for side, start in ((0, nz - 3), (1, 0)):
+            for k in range(5):
+                sz[side, pl.ds(3 * k, 3), :] = tz[k, pl.ds(start, 3), :]
 
     def own_turned():
         @pl.loop(0, nz // ROWS, unroll=4)
@@ -304,17 +308,23 @@
         peer = near(0, jnp.where(side == 0, 1, -1))
         return remote(raw.at[:, src], hx.at[side, :, dst], x_send, x_recv.at[p], peer)
 
+    def x_half(side, h):
+        src = jnp.where(side == 0, nx - 3, 2)
+        dst = jnp.where(side == 0, 0, 2)
+        rows = pl.ds(pl.multiple_of(h * half, ROWS), half)
+        peer = near(0, jnp.where(side == 0, 1, -1))
+        return remote(raw.at[:, src, rows], hx.at[side, :, dst, rows], x_send, x_recv.at[2 + h], peer)
+
     def x_near(side):
         src = raw.at[:, pl.ds(jnp.where(side == 0, nx - 3, 0), 3)]
-        return remote(src, hx.at[side], x_send, x_recv.at[3], near(0, jnp.where(side == 0, 1, -1)))
+        return remote(src, hx.at[side], x_send, x_recv.at[4], near(0, jnp.where(side == 0, 1, -1)))
 
     def y_copy(side):
         return remote(sy.at[side], hy.at[side], y_send, y_recv.at[side], near(1, 1 - 2 * side))
 
     def z_copies():
-        for side, start in ((0, nz - ROWS), (1, 0)):
-            src = tz.at[:, pl.ds(start, ROWS), :]
-            remote(src, hz.at[side], z_send, z_recv, near(2, 1 - 2 * side)).start()
+        for side in range(2):
+            remote(sz.at[side], hz.at[side], z_send, z_recv, near(2, 1 - 2 * side)).start()
 
     def allow(which, peer):
         pl.semaphore_signal(permit.at[which], inc=1, device_id=peer, device_id_type=MESH)
@@ -325,8 +335,10 @@
     else:
         for copy in exchange(0):
             copy.start()
-    for p in range(3):
+    for p in range(2):
         x_far(1 - odd, p).start()
+    for h in range(2):
+        x_half(1 - odd, h).start()
     x_near(odd).start()
     if star:
         pl.when(jnp.logical_not(ends[0]))(lambda: allow(0, near(1, -1)))
@@ -357,6 +369,24 @@
     lax.fori_loop(first, inside // 2, z_pair, 0)
     if inside % 2:
         z_face(inside)
+    pairs_of(lambda q: y_face(q // (tiles - 2), lax.rem(q, tiles - 2) + 1), 0, nx * (tiles - 2))
+
+    def x_cells(side, p, start, rows):
+        j = jnp.where(side == 0, 2 - p, p)
+        base = jnp.where(side == 0, 2 - p, nx + 3 + p) * ny
+        for t in range(rows // ROWS):
+            r = pl.multiple_of(start + t * ROWS, ROWS)
+            rho, v1, v2, v3, pr = [hx[side, k, j, pl.ds(r, ROWS), :] for k in range(5)]
+            basis = cell_basis(scale * rho, (v1, v2, v3), scale * pr)
+            put_cells(cx, pl.multiple_of(base + r, ROWS), cell_arrays(basis, FIRST))
+
+    def x_faces(start, number):
+        def x_face(q):
+            r = pl.multiple_of(start + q * ROWS, ROWS)
+            face_tile(cx, gx, r, ny, r)
+
+        pairs_of(x_face, 0, number)
+
     if star:
         needed = jnp.where(last, 0, 1) + jnp.where(lower, 1, 0)
         pl.when(needed > 0)(lambda: pl.semaphore_wait(permit.at[0], needed))
@@ -364,31 +394,11 @@
         pl.when(jnp.logical_not(last))(lambda: y_copy(0).start())
     if not star:
         next_top(0)
-
-    pairs_of(lambda q: y_face(q // (tiles - 2), lax.rem(q, tiles - 2) + 1), 0, nx * (tiles - 2))
-
-    if not star:
         next_top(1)
 
-    def x_plane(side, p):
-        j = jnp.where(side == 0, 2 - p, p)
-        base = jnp.where(side == 0, 2 - p, nx + 3 + p) * ny
-        for t in range(tiles):
-            r = t * ROWS
-            rho, v1, v2, v3, pr = [hx[side, k, j, pl.ds(r, ROWS), :] for k in range(5)]
-            basis = cell_basis(scale * rho, (v1, v2, v3), scale * pr)
-            put_cells(cx, pl.multiple_of(base + r, ROWS), cell_arrays(basis, FIRST))
-
-    def x_faces(start, number):
-        def x_face(q):
-            r = pl.multiple_of(start * ny + q * ROWS, ROWS)
-            face_tile(cx, gx, r, ny, r)
-
-        pairs_of(x_face, 0, number * tiles)
-
     x_near(1 - odd).wait_recv()
-    pl.loop(0, 3)(lambda p: x_plane(1 - odd, p))
-    x_faces(jnp.where(odd == 1, 0, 3), nx - 2)
+    pl.loop(0, 3)(lambda p: x_cells(1 - odd, p, 0, ny))
+    x_faces(jnp.where(odd == 1, 0, 3) * ny, (nx - 2) * tiles)
 
     if star:
         @pl.when(ends[0])
@@ -397,8 +407,8 @@
             y_copy(1).start()
 
     remote(hz, hz, z_send, z_recv, near(2, 1)).wait_recv()
-    for side, row in ((0, 0), (1, nz + ROWS)):
-        rho, v1, v2, v3, p = [hz[side, k] for k in range(5)]
+    for side, row in ((0, ROWS - 3), (1, nz + ROWS)):
+        rho, v1, v2, v3, p = [hz[side, pl.ds(3 * k, 3), :] for k in range(5)]
         put_cells(cz, row, cell_arrays(cell_basis(scale * rho, (v1, v2, v3), scale * p), THIRD))
 
     @pl.loop(0, 3)
@@ -419,25 +429,17 @@
 
     def x_next(p):
         x_far(odd, p).wait_recv()
-        x_plane(odd, p)
-        x_faces(jnp.where(odd == 1, nx - 2 + p, 2 - p), 1)
-
-    pl.when(last)(lambda: y_side(0))
-    pl.when(jnp.logical_not(last))(lambda: y_side(1))
-    pl.loop(0, 2)(x_next)
-    pl.when(last)(lambda: y_side(1))
-    pl.when(jnp.logical_not(last))(lambda: y_side(0))
-    face_tile(cy, gy, ny + 5, 1, ny, nx, ypad)
-
-    @pl.loop(0, nx)
-    def _(i):
-        for t in range(tiles):
-            r = t * ROWS
-            row = pl.multiple_of(i * ny + r, ROWS)
-            yrow = pl.multiple_of(i * ypad + r, ROWS)
-            for field, k in enumerate((0, 2, 1, 3, 4)):
-                turn = gy[k, pl.ds(yrow + 1, ROWS), :] - gy[k, pl.ds(yrow, ROWS), :]
-                acc[field, pl.ds(row, ROWS), :] = acc[field, pl.ds(row, ROWS), :] + turn
+        x_cells(odd, p, 0, ny)
+        x_faces(jnp.where(odd == 1, nx - 2 + p, 2 - p) * ny, tiles)
+
+    def x_end(h):
+        x_half(odd, h).wait_recv()
+        x_cells(odd, 2, h * half, half)
+        x_faces(jnp.where(odd == 1, nx, 0) * ny + h * half, half // ROWS)
+
+    def set_factor(best):
+        largest = jnp.max(best, axis=1, keepdims=True)
+        top[4] = jnp.broadcast_to((cfl_number / (12.0 * scale)) / largest, (1, lanes))
 
     def gather(k):
         @pl.when(rank == roots[k])
@@ -445,19 +447,47 @@
             slots(devices - 1, top_send, top_recv).wait_recv()
             best = jnp.max(got[...], axis=0)
             top[1] = best
-            top[2] = best
             if k == 1:
                 for d in reversed(range(devices)):
                     if d not in roots:
                         cast(d).start()
-
-    if star:
-        gather(1)
-    else:
-        next_top(2)
-    x_next(2)
-    if star:
-        gather(0)
+            set_factor(best)
+
+    pl.when(last)(lambda: y_side(0))
+    pl.when(jnp.logical_not(last))(lambda: y_side(1))
+    turn = jnp.where(rank == roots[1], 1, 2) if star else 2
+
+    def y_end():
+        face_tile(cy, gy, ny + 5, 1, ny, nx, ypad)
+
+    pl.when(jnp.logical_not(last))(y_end)
+
+    def y_rest():
+        @pl.when(last)
+        def _():
+            y_side(1)
+            y_end()
+
+        pl.when(jnp.logical_not(last))(lambda: y_side(0))
+
+        @pl.loop(0, nx)
+        def _(i):
+            for t in range(tiles):
+                r = t * ROWS
+                row = pl.multiple_of(i * ny + r, ROWS)
+                yrow = pl.multiple_of(i * ypad + r, ROWS)
+                for field, k in enumerate((0, 2, 1, 3, 4)):
+                    turn = gy[k, pl.ds(yrow + 1, ROWS), :] - gy[k, pl.ds(yrow, ROWS), :]
+                    acc[field, pl.ds(row, ROWS), :] = acc[field, pl.ds(row, ROWS), :] + turn
+
+    @pl.loop(0, 3)
+    def _(p):
+        pl.when(p == turn)(y_rest)
+        if star:
+            pl.when(p == 1)(lambda: gather(1))
+        pl.when(p < 2)(lambda: x_next(p))
+
+    pl.loop(0, 2)(x_end)
 
     @pl.loop(0, nx)
     def _(i):
@@ -468,9 +498,16 @@
                 acc[field, pl.ds(row, ROWS), :] = acc[field, pl.ds(row, ROWS), :] + turn
 
     if star:
-        pl.when(jnp.logical_not(root))(lambda: cast(0).wait_recv())
-    largest = jnp.max(top[2 if star else 3], axis=(0, 1), keepdims=True)
-    factor = jnp.broadcast_to((cfl_number / (12.0 * scale)) / largest, (ROWS, lanes))
+        gather(0)
+
+        @pl.when(jnp.logical_not(root))
+        def _():
+            cast(0).wait_recv()
+            set_factor(top[2])
+    else:
+        next_top(2)
+        set_factor(top[3])
+    factor = jnp.broadcast_to(top[4], (ROWS, lanes))
 
     @pl.loop(0, nx)
     def _(i):
@@ -516,12 +553,13 @@
             pltpu.VMEM((2, 5, 3, ny, nz), f32),
             pltpu.VMEM((2, edge, nz), f32),
             pltpu.VMEM((2, edge, nz), f32),
-            pltpu.VMEM((2, 5, ROWS, nrow), f32),
-            pltpu.VMEM((4, 1, nz), f32),
+            pltpu.VMEM((2, 2 * ROWS, nrow), f32),
+            pltpu.VMEM((2, 2 * ROWS, nrow), f32),
+            pltpu.VMEM((5, 1, nz), f32),
             pltpu.VMEM((slots, 1, nz), f32),
             pltpu.SemaphoreType.DMA,
             pltpu.SemaphoreType.DMA,
-            pltpu.SemaphoreType.DMA((4,)),
+            pltpu.SemaphoreType.DMA((5,)),
             pltpu.SemaphoreType.DMA,
             pltpu.SemaphoreType.DMA((2,)),
             pltpu.SemaphoreType.DMA,

time: 11.8 us -> 11.1 us (0.941)
  Pallas kernels: 11 us -> 10.3 us
    pallas_call x1, Pallas kernels: 11 us -> 10.3 us  [local(): pl.pallas_call(functools.partial(kernel, counts), out_shape=pltpu.VMEM((5...]
where the time goes in v3:
time: 11.1 us; the launch traced here: 11 us
  Pallas kernels  10.3 us (93%)
  local copies, waits for them, and re-layouts  0.73 us (7%)
    pallas_call x1, Pallas kernels, local(): pl.pallas_call(functools.partial(kernel, counts), out_shape=pltpu.VMEM((5...  10.3 us
    unnamed x1, local copies, waits for them, and re-layouts  0.73 us

profile of v3, /device:TPU:1, one launch (start us, length us, event | category | flops | bytes accessed | tf_op | source)
XLA Modules:
  0.0 11.0 jit_solution(5793185447734394920)
XLA Ops:
  0.0 10.3 %shard_map.37 = f32[5,4,32,128]{3,2,1,0:T(8,128)S(1)} custom-call(f32[4,32,128]{2,1,0:T(8,128)} %den_in.1, f32[3,4,32,128]{3,2,1,0:T(8,128)} %vel_in.1, f32[4,32,128]{2,1,0:T(8,128)} %pre_in.1), custom_call_target="tpu_custom_call" | custom-call | tf_op jit(solution)/shard_map/pallas_call | solution.py:538
  10.3 0.7 %copy.5 = f32[5,4,32,128]{3,2,1,0:T(8,128)} copy(f32[5,4,32,128]{3,2,1,0:T(8,128)S(1)} %shard_map.37) | data formatting | bytes 655360

commit v4 on v3

--- a/solution.py
+++ b/solution.py
@@ -133,26 +133,27 @@
 def kernel(
     counts, den_in, vel_in, pre_in, out,
     raw, cx, cy, cz, gx, gy, gz, acc, tz, hx, sy, hy, sz, hz, top, got,
-    in_sem, x_send, x_recv, y_send, y_recv, z_send, z_recv, top_send, top_recv, cast_send, cast_recv, permit,
+    x_send, x_recv, edge_send, y_recv, z_recv, top_send, top_recv, cast_recv, permit,
 ):
     nx, ny, lanes = raw.shape[1:]
     nrow = nx * ny
     nz = lanes
     tiles = ny // ROWS
     ypad = ny + 2 * ROWS
-    half = ny // 2
+    half, quarter = ny // 2, ny // 4
     devices = math.prod(counts)
     star = is_star(counts)
 
     pairs = ((den_in, raw.at[0]), (vel_in, raw.at[pl.ds(1, 3)]), (pre_in, raw.at[4]))
     for a, b in pairs:
-        pltpu.make_async_copy(a, b, in_sem).start()
+        pltpu.make_async_copy(a, b, x_send).start()
 
     me = [lax.axis_index(a) for a in AXES]
     rank = (me[0] * counts[1] + me[1]) * counts[2] + me[2]
     roots = (0, counts[1] * counts[2])
     root = jnp.logical_and(me[0] <= 1, jnp.logical_and(me[1] == 0, me[2] == 0))
     odd = lax.rem(me[0], 2)
+    early = jnp.logical_or(root, me[0] == 1)
     last = me[1] == counts[1] - 1
 
     def device(d):
@@ -192,7 +193,7 @@
         for _, peer in peers:
             greet(peer)
 
-    pltpu.make_async_copy(raw, raw, in_sem).wait()
+    pltpu.make_async_copy(raw, raw, x_send).wait()
 
     def speeds(i, best):
         for t in range(tiles):
@@ -208,6 +209,7 @@
     top[0] = own
     if star:
         got[rank] = own
+        top[1] = own
 
     def own_cells():
         @pl.loop(0, nx)
@@ -219,11 +221,13 @@
                 put_cells(cx, pl.multiple_of((3 + i) * ny + r, ROWS), cell_arrays(basis, FIRST))
                 put_cells(cy, pl.multiple_of(i * ypad + ROWS + r, ROWS), cell_arrays(basis, SECOND))
 
-    def stage():
+    def stage_rows():
         for side, start in ((0, ny - 3), (1, 0)):
             for i in range(nx):
                 for k in range(5):
                     sy[side, pl.ds(3 * (k * nx + i), 3), :] = raw[k, i, pl.ds(start, 3), :]
+
+    def stage_turned():
         for k in range(5):
             tz[k] = raw[k].reshape(nrow, nz).T
         for side, start in ((0, nz - 3), (1, 0)):
@@ -254,18 +258,23 @@
         if number % 2:
             body(start + number - 1)
 
+    def z_pair(q, carry):
+        z_face(1 + 2 * q)
+        z_face(2 + 2 * q)
+        return carry
+
     inside = nz // ROWS - 2
     first = 0
     if star:
-        ahead = min(AHEAD, inside) // 2
-
-        @pl.when(root)
-        def _():
-            stage()
+        first = jnp.where(root, min(AHEAD, inside) // 2, jnp.where(early, 1, 0))
+
+        @pl.when(early)
+        def _():
+            stage_rows()
+            stage_turned()
             own_turned()
-            pairs_of(z_face, 1, 2 * ahead)
-
-        first = jnp.where(root, ahead, 0)
+            lax.fori_loop(0, first, z_pair, 0)
+
 
     pl.semaphore_wait(barrier, greeted)
 
@@ -278,7 +287,7 @@
         return remote(top.at[0], got.at[rank], top_send, top_recv, device(jnp.int32(roots[k])))
 
     def cast(d):
-        return remote(top.at[1], top.at[2], cast_send, cast_recv, device(jnp.int32(d)))
+        return remote(top.at[1], top.at[2], top_send, cast_recv, device(jnp.int32(d)))
 
     def slots(number, send, recv):
         part = got.at[pl.ds(0, number)]
@@ -302,29 +311,29 @@
             for copy in exchange(axis + 1):
                 copy.start()
 
-    def x_far(side, p):
+    def x_piece(side, p, start, rows, slot):
         src = jnp.where(side == 0, nx - 1 - p, p)
         dst = jnp.where(side == 0, 2 - p, p)
+        part = pl.ds(pl.multiple_of(start, ROWS), rows)
         peer = near(0, jnp.where(side == 0, 1, -1))
-        return remote(raw.at[:, src], hx.at[side, :, dst], x_send, x_recv.at[p], peer)
-
-    def x_half(side, h):
-        src = jnp.where(side == 0, nx - 3, 2)
-        dst = jnp.where(side == 0, 0, 2)
-        rows = pl.ds(pl.multiple_of(h * half, ROWS), half)
-        peer = near(0, jnp.where(side == 0, 1, -1))
-        return remote(raw.at[:, src, rows], hx.at[side, :, dst, rows], x_send, x_recv.at[2 + h], peer)
+        return remote(raw.at[:, src, part], hx.at[side, :, dst, part], x_send, x_recv.at[slot], peer)
+
+    def x_half(side, q):
+        return x_piece(side, lax.div(q, 2), lax.rem(q, 2) * half, half, q)
+
+    def x_tail(side, q):
+        return x_piece(side, 2, half + q * quarter, quarter, 5 + q)
 
     def x_near(side):
         src = raw.at[:, pl.ds(jnp.where(side == 0, nx - 3, 0), 3)]
-        return remote(src, hx.at[side], x_send, x_recv.at[4], near(0, jnp.where(side == 0, 1, -1)))
+        return remote(src, hx.at[side], x_send, x_recv.at[7], near(0, jnp.where(side == 0, 1, -1)))
 
     def y_copy(side):
-        return remote(sy.at[side], hy.at[side], y_send, y_recv.at[side], near(1, 1 - 2 * side))
+        return remote(sy.at[side], hy.at[side], edge_send, y_recv.at[side], near(1, 1 - 2 * side))
 
     def z_copies():
         for side in range(2):
-            remote(sz.at[side], hz.at[side], z_send, z_recv, near(2, 1 - 2 * side)).start()
+            remote(sz.at[side], hz.at[side], edge_send, z_recv, near(2, 1 - 2 * side)).start()
 
     def allow(which, peer):
         pl.semaphore_signal(permit.at[which], inc=1, device_id=peer, device_id_type=MESH)
@@ -335,40 +344,39 @@
     else:
         for copy in exchange(0):
             copy.start()
-    for p in range(2):
-        x_far(1 - odd, p).start()
-    for h in range(2):
-        x_half(1 - odd, h).start()
+    for q in range(5):
+        x_half(1 - odd, jnp.int32(q)).start()
+    for q in range(2):
+        x_tail(1 - odd, q).start()
     x_near(odd).start()
     if star:
         pl.when(jnp.logical_not(ends[0]))(lambda: allow(0, near(1, -1)))
         pl.when(jnp.logical_not(lower))(lambda: allow(0, near(2, -1)))
         pl.when(last)(lambda: allow(1, near(1, 1)))
 
-        @pl.when(jnp.logical_not(root))
-        def _():
-            stage()
-
+        pl.when(jnp.logical_not(early))(stage_rows)
         pl.when(last)(lambda: y_copy(0).start())
         pl.when(jnp.logical_not(ends[0]))(lambda: y_copy(1).start())
+        pl.when(jnp.logical_not(early))(stage_turned)
         pl.when(jnp.logical_not(lower))(z_copies)
-        pl.when(jnp.logical_not(root))(own_turned)
+        pl.when(jnp.logical_not(early))(own_turned)
     else:
-        stage()
+        stage_rows()
+        stage_turned()
         z_copies()
         y_copy(0).start()
         y_copy(1).start()
         own_turned()
     own_cells()
 
-    def z_pair(q, carry):
-        z_face(1 + 2 * q)
-        z_face(2 + 2 * q)
-        return carry
-
     lax.fori_loop(first, inside // 2, z_pair, 0)
     if inside % 2:
         z_face(inside)
+    if star:
+        needed = jnp.where(last, 0, 1) + jnp.where(lower, 1, 0)
+        pl.when(needed > 0)(lambda: pl.semaphore_wait(permit.at[0], needed))
+        pl.when(lower)(z_copies)
+        pl.when(jnp.logical_not(last))(lambda: y_copy(0).start())
     pairs_of(lambda q: y_face(q // (tiles - 2), lax.rem(q, tiles - 2) + 1), 0, nx * (tiles - 2))
 
     def x_cells(side, p, start, rows):
@@ -387,11 +395,6 @@
 
         pairs_of(x_face, 0, number)
 
-    if star:
-        needed = jnp.where(last, 0, 1) + jnp.where(lower, 1, 0)
-        pl.when(needed > 0)(lambda: pl.semaphore_wait(permit.at[0], needed))
-        pl.when(lower)(z_copies)
-        pl.when(jnp.logical_not(last))(lambda: y_copy(0).start())
     if not star:
         next_top(0)
         next_top(1)
@@ -406,7 +409,7 @@
             pl.semaphore_wait(permit.at[1], 1)
             y_copy(1).start()
 
-    remote(hz, hz, z_send, z_recv, near(2, 1)).wait_recv()
+    remote(hz, hz, edge_send, z_recv, near(2, 1)).wait_recv()
     for side, row in ((0, ROWS - 3), (1, nz + ROWS)):
         rho, v1, v2, v3, p = [hz[side, pl.ds(3 * k, 3), :] for k in range(5)]
         put_cells(cz, row, cell_arrays(cell_basis(scale * rho, (v1, v2, v3), scale * p), THIRD))
@@ -427,15 +430,22 @@
 
         pairs_of(lambda i: y_face(i, (tiles - 1) * side), 0, nx)
 
-    def x_next(p):
-        x_far(odd, p).wait_recv()
-        x_cells(odd, p, 0, ny)
-        x_faces(jnp.where(odd == 1, nx - 2 + p, 2 - p) * ny, tiles)
-
-    def x_end(h):
-        x_half(odd, h).wait_recv()
-        x_cells(odd, 2, h * half, half)
-        x_faces(jnp.where(odd == 1, nx, 0) * ny + h * half, half // ROWS)
+    def x_next(q):
+        x_half(odd, q).wait_recv()
+        p, start = lax.div(q, 2), lax.rem(q, 2) * half
+        x_cells(odd, p, start, half)
+        x_faces(jnp.where(odd == 1, nx - 2 + p, 2 - p) * ny + start, half // ROWS)
+
+    def x_last(q):
+        x_cells(odd, 2, half + q * quarter, quarter)
+        x_faces(jnp.where(odd == 1, nx, 0) * ny + half + q * quarter, quarter // ROWS)
+
+    def x_turn(i):
+        for t in range(tiles):
+            row = pl.multiple_of(i * ny + t * ROWS, ROWS)
+            for field in range(5):
+                turn = gx[field, pl.ds(row + ny, ROWS), :] - gx[field, pl.ds(row, ROWS), :]
+                acc[field, pl.ds(row, ROWS), :] = acc[field, pl.ds(row, ROWS), :] + turn
 
     def set_factor(best):
         largest = jnp.max(best, axis=1, keepdims=True)
@@ -451,11 +461,10 @@
                 for d in reversed(range(devices)):
                     if d not in roots:
                         cast(d).start()
-            set_factor(best)
 
     pl.when(last)(lambda: y_side(0))
     pl.when(jnp.logical_not(last))(lambda: y_side(1))
-    turn = jnp.where(rank == roots[1], 1, 2) if star else 2
+    turn = jnp.where(rank == roots[1], 2, 4) if star else 4
 
     def y_end():
         face_tile(cy, gy, ny + 5, 1, ny, nx, ypad)
@@ -480,26 +489,28 @@
                     turn = gy[k, pl.ds(yrow + 1, ROWS), :] - gy[k, pl.ds(yrow, ROWS), :]
                     acc[field, pl.ds(row, ROWS), :] = acc[field, pl.ds(row, ROWS), :] + turn
 
-    @pl.loop(0, 3)
-    def _(p):
-        pl.when(p == turn)(y_rest)
+    @pl.loop(0, 5)
+    def _(q):
+        @pl.when(q == 4)
+        def _():
+            pl.loop(0, nx - 1)(lambda k: x_turn(k + 1 - odd))
+
+        pl.when(q == turn)(y_rest)
         if star:
-            pl.when(p == 1)(lambda: gather(1))
-        pl.when(p < 2)(lambda: x_next(p))
-
-    pl.loop(0, 2)(x_end)
-
-    @pl.loop(0, nx)
-    def _(i):
-        for t in range(tiles):
-            row = pl.multiple_of(i * ny + t * ROWS, ROWS)
-            for field in range(5):
-                turn = gx[field, pl.ds(row + ny, ROWS), :] - gx[field, pl.ds(row, ROWS), :]
-                acc[field, pl.ds(row, ROWS), :] = acc[field, pl.ds(row, ROWS), :] + turn
-
+            pl.when(q == 3)(lambda: gather(1))
+        x_next(q)
+
+    x_tail(odd, 0).wait_recv()
+    x_last(0)
     if star:
         gather(0)
-
+    x_tail(odd, 1).wait_recv()
+    if star:
+        set_factor(top[1])
+    x_last(1)
+    x_turn(odd * (nx - 1))
+
+    if star:
         @pl.when(jnp.logical_not(root))
         def _():
             cast(0).wait_recv()
@@ -519,12 +530,12 @@
                 out[field, i, pl.ds(r, ROWS), :] = (1.0 / scale) * state - factor * acc[field, pl.ds(row, ROWS), :]
 
     if star:
-        pl.when(root)(lambda: slots(1, top_send, top_recv).wait_send())
+        pl.when(rank == roots[0])(lambda: slots(1, top_send, top_recv).wait_send())
+        pl.when(rank == roots[1])(lambda: slots(devices - 1, top_send, top_recv).wait_send())
         pl.when(jnp.logical_not(root))(lambda: slots(2, top_send, top_recv).wait_send())
-        pl.when(rank == roots[1])(lambda: slots(devices - 2, cast_send, cast_recv).wait_send())
     remote(hx, hx, x_send, x_recv.at[0], near(0, 1)).wait_send()
-    remote(sy, sy, y_send, y_recv.at[0], near(1, 1)).wait_send()
-    remote(hz, hz, z_send, z_recv, near(2, 1)).wait_send()
+    edges = cx.at[0, pl.ds(0, 2 * (sy.shape[1] + sz.shape[1]))]
+    remote(edges, edges, edge_send, z_recv, near(2, 1)).wait_send()
 
 
 def local(counts, density, velocity, pressure):
@@ -558,14 +569,11 @@
             pltpu.VMEM((5, 1, nz), f32),
             pltpu.VMEM((slots, 1, nz), f32),
             pltpu.SemaphoreType.DMA,
-            pltpu.SemaphoreType.DMA,
-            pltpu.SemaphoreType.DMA((5,)),
+            pltpu.SemaphoreType.DMA((8,)),
             pltpu.SemaphoreType.DMA,
             pltpu.SemaphoreType.DMA((2,)),
             pltpu.SemaphoreType.DMA,
-            pltpu.SemaphoreType.DMA,
             *hands,
-            pltpu.SemaphoreType.DMA,
             pltpu.SemaphoreType.DMA,
             pltpu.SemaphoreType.REGULAR((2,)),
         ],

time: 11.1 us -> 10.9 us (0.982)
  Pallas kernels: 10.3 us -> 9.97 us
    pallas_call x1, Pallas kernels: 10.3 us -> 9.97 us  [local(): pl.pallas_call(functools.partial(kernel, counts), out_shape=pltpu.VMEM((5...]
where the time goes in v4:
time: 10.9 us; the launch traced here: 10.7 us
  Pallas kernels  9.97 us (91%)
  local copies, waits for them, and re-layouts  0.73 us (7%)
    pallas_call x1, Pallas kernels, local(): pl.pallas_call(functools.partial(kernel, counts), out_shape=pltpu.VMEM((5...  9.97 us
    unnamed x1, local copies, waits for them, and re-layouts  0.73 us

profile of v4, /device:TPU:1, one launch (start us, length us, event | category | flops | bytes accessed | tf_op | source)
XLA Modules:
  0.0 10.7 jit_solution(12493552538777853986)
XLA Ops:
  0.0 10.0 %shard_map.37 = f32[5,4,32,128]{3,2,1,0:T(8,128)S(1)} custom-call(f32[4,32,128]{2,1,0:T(8,128)} %den_in.1, f32[3,4,32,128]{3,2,1,0:T(8,128)} %vel_in.1, f32[4,32,128]{2,1,0:T(8,128)} %pre_in.1), custom_call_target="tpu_custom_call" | custom-call | tf_op jit(solution)/shard_map/pallas_call | solution.py:549
  10.0 0.7 %copy.5 = f32[5,4,32,128]{3,2,1,0:T(8,128)} copy(f32[5,4,32,128]{3,2,1,0:T(8,128)S(1)} %shard_map.37) | data formatting | bytes 655360

commit v5 on v4

--- a/solution.py
+++ b/solution.py
@@ -144,9 +144,12 @@
     devices = math.prod(counts)
     star = is_star(counts)
 
-    pairs = ((den_in, raw.at[0]), (vel_in, raw.at[pl.ds(1, 3)]), (pre_in, raw.at[4]))
-    for a, b in pairs:
-        pltpu.make_async_copy(a, b, x_send).start()
+    for i in range(0, nx, 1):
+        part = pl.ds(i, 1)
+        pltpu.make_async_copy(den_in.at[part], raw.at[0, part], x_send).start()
+        for k in range(3):
+            pltpu.make_async_copy(vel_in.at[k, part], raw.at[1 + k, part], x_send).start()
+        pltpu.make_async_copy(pre_in.at[part], raw.at[4, part], x_send).start()
 
     me = [lax.axis_index(a) for a in AXES]
     rank = (me[0] * counts[1] + me[1]) * counts[2] + me[2]

time: 10.9 us -> 10.8 us (level)
  no operation moved by 1% of the time
where the time goes in v5:
time: 10.8 us; the launch traced here: 10.7 us
  Pallas kernels  9.92 us (92%)
  local copies, waits for them, and re-layouts  0.73 us (7%)
    pallas_call x1, Pallas kernels, local(): pl.pallas_call(functools.partial(kernel, counts), out_shape=pltpu.VMEM((5...  9.92 us
    unnamed x1, local copies, waits for them, and re-layouts  0.73 us

profile of v5, /device:TPU:1, one launch (start us, length us, event | category | flops | bytes accessed | tf_op | source)
XLA Modules:
  0.0 10.7 jit_solution(13202413658937764779)
XLA Ops:
  0.0 9.9 %shard_map.37 = f32[5,4,32,128]{3,2,1,0:T(8,128)S(1)} custom-call(f32[4,32,128]{2,1,0:T(8,128)} %den_in.1, f32[3,4,32,128]{3,2,1,0:T(8,128)} %vel_in.1, f32[4,32,128]{2,1,0:T(8,128)} %pre_in.1), custom_call_target="tpu_custom_call" | custom-call | tf_op jit(solution)/shard_map/pallas_call | solution.py:552
  9.9 0.7 %copy.5 = f32[5,4,32,128]{3,2,1,0:T(8,128)} copy(f32[5,4,32,128]{3,2,1,0:T(8,128)S(1)} %shard_map.37) | data formatting | bytes 655360
